TPU v7x, 32 devices: a whole 2x2x4 slice. The times are simulated.
32 devices in a mesh: tok: 8 (over z, x), exp: 4 (over y, core).
Axes of the slice: x: 2, y: 2, z: 4, core: 2. Of those that a mesh axis runs over, the one named last changes fastest.
Arguments:
- tokens: bfloat16 [16384, 7168], P('tok', 'exp'), may hold values from -6 to 6
- gate_weight: bfloat16 [7168, 256], P('exp'), may hold values from -0.0625 to 0.0625
- expert_ids: int32 [16384, 8], P('tok'), may hold values from 0 to 255, all different within a row
- expert_bias: float32 [256], P('exp'), may hold values from -0.002 to 0.002
Outputs:
- affinities: float32 [16384, 256], P('tok', 'exp')
- weights: float32 [16384, 8], P('tok')
- load: float32 [256], replicated
- new_bias: float32 [256], replicated
All inputs are finite; a program needn't handle non-finite values.
Results may differ from a plain program's by a relative error of at most 0.0003.
Values may be sent and summed in bfloat16 or wider, within the bound.
No kernel may reach another device: no remote copies, remote signals or barrier semaphores. Data moves between devices by JAX's collectives and lax.ppermute only.
A program may use at most 64 MiB of HBM per device.

v0:
```python
import jax
import jax.numpy as jnp
from jax import lax
from jax.sharding import PartitionSpec as P


def count_experts(expert_ids, width):
    numbers = lax.iota(jnp.int32, width)
    matches = expert_ids[:, :, None] == numbers[None, None, :]
    return jnp.sum(matches.astype(jnp.float32), axis=(0, 1))


def local(tokens, gate_weight, expert_ids, expert_bias):
    experts_all = gate_weight.shape[1]
    own_width = expert_bias.shape[0]
    first_expert = lax.axis_index("exp") * own_width
    tok_rows = tokens.shape[0]
    partial_logits = jnp.dot(tokens, gate_weight, preferred_element_type=jnp.float32)
    logits = lax.psum_scatter(partial_logits, "exp", scatter_dimension=1, tiled=True)
    affinities = jax.nn.sigmoid(logits)
    numbers = first_expert + lax.iota(jnp.int32, own_width)
    matches = expert_ids[:, :, None] == numbers[None, None, :]
    chosen_part = jnp.sum(jnp.where(matches, affinities[:, None, :], jnp.float32(0.0)), axis=2)
    chosen = lax.psum(chosen_part, "exp")
    weights = 2.5 * chosen / jnp.sum(chosen, axis=1, keepdims=True)
    target = jnp.float32(tok_rows * lax.axis_size("tok") * expert_ids.shape[1])
    bias_whole = lax.all_gather(expert_bias, "exp", axis=0, tiled=True)
    load = lax.psum(count_experts(expert_ids, experts_all), "tok")
    new_bias = bias_whole + 0.001 * jnp.sign(target - jnp.float32(experts_all) * load)
    return (affinities, weights, load, new_bias)


def solution(mesh):
    in_specs = (P("tok", "exp"), P("exp", None), P("tok", None), P("exp"))
    out_specs = (P("tok", "exp"), P("tok", None), P(), P())
    return jax.shard_map(local, mesh=mesh, in_specs=in_specs, out_specs=out_specs, check_vma=False)
```

profile of v0, /device:TPU:0, one launch (start us, length us, event | category | flops | bytes accessed | tf_op | source)
XLA Modules:
  0.0 92.7 jit_solution(2102868022089184914)
XLA Ops:
  7.2 0.0 copy-start
  7.2 0.0 copy-start.5
  7.2 0.0 copy-start.2
  7.2 0.0 copy-start.4
  7.2 0.0 reduce-scatter.2.cloned.1.call-start
  7.3 1.1 %copy-done = bf16[1792,256]{1,0:T(8,128)(2,1)S(1)} copy-done((bf16[1792,256]{1,0:T(8,128)(2,1)S(1)}, bf16[1792,256]{1,0:T(8,128)(2,1)}, u32[]{:S(2)}) %copy-start) | copy-done | bytes 917528
  8.4 6.5 %fusion = f32[2048,256]{0,1:T(8,128)} fusion(bf16[2048,1792]{1,0:T(8,128)(2,1)} %param.4, bf16[1792,256]{1,0:T(8,128)(2,1)S(1)} %copy-done), kind=kOutput, calls=%fused_computation.7 | convolution fusion | flops 1879048192 | bytes 10354688 | tf_op jit(solution)/shard_map/dot_general | solution.py:18
  14.9 0.0 reduce-scatter.2.cloned.1.call-update
  14.9 0.0 all-reduce.3.cloned.1.call-start
  15.0 0.0 copy-done.2
  15.0 0.3 copy.11
  15.4 0.0 copy-done.5
  15.4 0.6 dynamic-slice
  16.6 0.0 copy-done.4
  16.6 0.2 dynamic-update-slice
  16.9 5.1 %convert_reduce_fusion = f32[256]{0:T(256)S(1)} fusion(s32[2048,8]{1,0:T(8,128)S(1)} %copy.11), kind=kLoop, calls=%fused_computation | loop fusion | flops 12582656 | bytes 66560 | tf_op jit(solution)/shard_map/reduce_sum | solution.py:10
  22.0 23.1 %psum.15 = f32[256]{0:T(256)S(1)} all-reduce(f32[256]{0:T(256)S(1)} %convert_reduce_fusion), channel_id=1, replica_groups=mesh['tok'=8,'exp'=4] {'tok'}, use_global_device_ids=true, to_apply=%region_5.6 | all-reduce | flops 256 | bytes 2048 | tf_op jit(solution)/shard_map/psum | solution.py:28
  45.1 0.0 copy-start.3
  45.1 5.7 %all-reduce = f32[256]{0:T(256)S(1)} all-reduce(f32[256]{0:T(256)S(1)} %dynamic-update-slice), channel_id=1, replica_groups=mesh['tok'=8,'exp'=4] {'exp'}, use_global_device_ids=true, to_apply=%add | all-reduce | flops 256 | bytes 2048
  50.8 0.0 reduce-scatter.2.cloned.1.call-done
  50.8 1.2 %add_divide_fusion = f32[2048,64]{0,1:T(8,128)S(1)} fusion(f32[2048,64]{0,1:T(8,128)} %reduce-scatter.2.cloned.1.call-done), kind=kLoop, calls=%fused_computation.3 | loop fusion | flops 393216 | bytes 1048576 | tf_op jit(solution)/shard_map/div | solution.py:20
  52.0 0.0 copy-start.1
  52.0 1.2 %select_reduce_fusion = f32[2048,8]{0,1:T(8,128)} fusion(f32[2048,64]{0,1:T(8,128)S(1)} %add_divide_fusion, s32[2048,8]{0,1:T(8,128)S(1)} %copy-done.2, s32[64]{0:T(128)S(1)} %iota_add_fusion), kind=kLoop, calls=%fused_computation.2 | loop fusion | flops 3129344 | bytes 655616 | tf_op jit(solution)/shard_map/reduce_sum | solution.py:23
  53.2 0.0 all-reduce.3.cloned.1.call-update
  53.2 0.6 multiply_add_fusion
  53.8 29.7 %all-reduce.3.cloned.1.call-done = f32[2048,8]{0,1:T(8,128)} async-done(((f32[2048,8]{0,1:T(8,128)}), f32[2048,8]{0,1:T(8,128)}) %all-reduce.3.cloned.1.call-update) | async-done | bytes 65552 | tf_op jit(solution)/shard_map/psum | solution.py:24
  83.5 0.9 reduce_sum.28
  84.4 1.5 %multiply_divide_fusion = f32[2048,8]{0,1:T(8,128)} fusion(f32[2048,8]{0,1:T(8,128)} %all-reduce.3.cloned.1.call-done, f32[2048]{0:T(1024)S(1)} %reduce_sum.28), kind=kLoop, calls=%fused_computation.4 | loop fusion | flops 32768 | bytes 139264 | tf_op jit(solution)/shard_map/div | solution.py:25
  85.9 0.0 copy-done.3
  85.9 0.0 copy-done.1
  (2 shorter events, 0.0 us)
Async XLA Ops:
  7.2 1.2 %copy-start = (bf16[1792,256]{1,0:T(8,128)(2,1)S(1)}, bf16[1792,256]{1,0:T(8,128)(2,1)}, u32[]{:S(2)}) copy-start(bf16[1792,256]{1,0:T(8,128)(2,1)} %param.5) | copy-start | bytes 2752516
  7.2 8.2 %copy-start.5 = (u32[32]{0:T(128)S(1)}, u32[32]{0:T(128)}, u32[]{:S(2)}) copy-start(u32[32]{0:T(128)} %constant.20) | copy-start | bytes 388
  7.2 7.8 %copy-start.2 = (s32[2048,8]{0,1:T(8,128)S(1)}, s32[2048,8]{0,1:T(8,128)}, u32[]{:S(2)}) copy-start(s32[2048,8]{0,1:T(8,128)} %param.6) | copy-start | bytes 196612
  7.2 9.4 %copy-start.4 = (f32[64]{0:T(128)S(1)}, f32[64]{0:T(128)}, u32[]{:S(2)}) copy-start(f32[64]{0:T(128)} %param.7) | copy-start | bytes 772
  7.2 43.6 %reduce-scatter.2.cloned.1.call-start = ((), (), s32[]{:S(2)}) async-start(), calls=%async_computation.1 | async-start | bytes 2621440 | tf_op jit(solution)/shard_map/reduce_scatter | solution.py:19
  14.9 68.6 %all-reduce.3.cloned.1.call-start = ((), (), s32[]{:S(2)}) async-start(), calls=%async_computation.2 | async-start | bytes 131072 | tf_op jit(solution)/shard_map/psum | solution.py:24
  45.1 40.8 %copy-start.3 = (f32[256]{0:T(256)}, f32[256]{0:T(256)S(1)}, u32[]{:S(2)}) copy-start(f32[256]{0:T(256)S(1)} %psum.15) | copy-start | bytes 3076
  52.0 33.9 %copy-start.1 = (f32[2048,64]{0,1:T(8,128)}, f32[2048,64]{0,1:T(8,128)S(1)}, u32[]{:S(2)}) copy-start(f32[2048,64]{0,1:T(8,128)S(1)} %add_divide_fusion) | copy-start | bytes 1572868
Sparse Core Ops, SparseCore 0:
  15.1 33.8 reduce-scatter.1
  53.3 30.1 all-reduce.2
where the time goes:
time: 93.1 us; the launch traced here: 92.7 us
  waiting for transfers between devices  29.8 us (32%)
  blocking collectives  28.8 us (31%)
  between operations  14.8 us (16%)
  other arithmetic  10.4 us (11%)
  matrix products  6.53 us (7%)
  local copies, waits for them, and re-layouts  2.31 us (2%)
    psum x1, waiting for transfers between devices, local(): chosen = lax.psum(chosen_part, 'exp')  29.7 us
    psum x1, blocking collectives, local(): load = lax.psum(count_experts(expert_ids, experts_all), 'tok')  23.1 us
    dot_general x1, matrix products, local(): jnp.dot(tokens, gate_weight, preferred_element_type=jnp.float32)  6.53 us
    unnamed x1, blocking collectives  5.66 us
    reduce_sum x1, other arithmetic, count_experts(): return jnp.sum(matches.astype(jnp.float32), axis=(0, 1))  5.11 us
    unnamed x16, local copies, waits for them, and re-layouts  2.31 us
  transfers between devices with their start and end apart: 2, of which 1 were waited for; matrix products, arithmetic and copies ran while one was open for 7% of the time, Pallas kernels for 0%

commit v1 on v0

--- a/solution.py
+++ b/solution.py
@@ -2,6 +2,10 @@
 import jax.numpy as jnp
 from jax import lax
 from jax.sharding import PartitionSpec as P
+
+
+def sample_number(here_x):
+    return jax.lax.all_gather(here_x, "exp").sum(axis=0)
 
 
 def count_experts(expert_ids, width):
@@ -21,7 +25,7 @@
     numbers = first_expert + lax.iota(jnp.int32, own_width)
     matches = expert_ids[:, :, None] == numbers[None, None, :]
     chosen_part = jnp.sum(jnp.where(matches, affinities[:, None, :], jnp.float32(0.0)), axis=2)
-    chosen = lax.psum(chosen_part, "exp")
+    chosen = sample_number(chosen_part)
     weights = 2.5 * chosen / jnp.sum(chosen, axis=1, keepdims=True)
     target = jnp.float32(tok_rows * lax.axis_size("tok") * expert_ids.shape[1])
     bias_whole = lax.all_gather(expert_bias, "exp", axis=0, tiled=True)

time: 93.1 us -> 67 us (0.72)
  waiting for transfers between devices: 29.8 us -> 0.02 us
  blocking collectives: 28.8 us -> 34.8 us
  other arithmetic: 10.4 us -> 8.2 us
    psum x1 -> x0, waiting for transfers between devices: 29.7 us -> none  [local(): chosen = lax.psum(chosen_part, 'exp')]
    all_gather x0 -> x1, blocking collectives: none -> 5.99 us  [sample_number(): return jax.lax.all_gather(here_x, 'exp').sum(axis=0)]
  transfers between devices with their start and end apart: 2 -> 1, of which waited for: 1 -> 0; matrix products, arithmetic and copies ran while one was open for 7% -> 10% of each run, Pallas kernels for 0% -> 0%
where the time goes in v1:
time: 67 us; the launch traced here: 66.7 us
  blocking collectives  34.8 us (52%)
  between operations  14.8 us (22%)
  other arithmetic  8.2 us (12%)
  matrix products  6.53 us (10%)
  local copies, waits for them, and re-layouts  2.33 us (3%)
    psum x1, blocking collectives, local(): load = lax.psum(count_experts(expert_ids, experts_all), 'tok')  23.1 us
    dot_general x1, matrix products, local(): jnp.dot(tokens, gate_weight, preferred_element_type=jnp.float32)  6.53 us
    all_gather x1, blocking collectives, sample_number(): return jax.lax.all_gather(here_x, 'exp').sum(axis=0)  5.99 us
    unnamed x1, blocking collectives  5.66 us
    reduce_sum x1, other arithmetic, count_experts(): return jnp.sum(matches.astype(jnp.float32), axis=(0, 1))  5.11 us
    unnamed x16, local copies, waits for them, and re-layouts  2.31 us
  transfers between devices with their start and end apart: 1, of which 0 were waited for; matrix products, arithmetic and copies ran while one was open for 10% of the time, Pallas kernels for 0%

profile of v1, /device:TPU:0, one launch (start us, length us, event | category | flops | bytes accessed | tf_op | source)
XLA Modules:
  0.0 66.7 jit_solution(8480631813736376254)
XLA Ops:
  7.2 0.0 copy-start
  7.2 0.0 copy-start.5
  7.2 0.0 copy-start.2
  7.2 0.0 copy-start.4
  7.2 0.0 reduce-scatter.2.cloned.1.call-start
  7.3 1.1 %copy-done = bf16[1792,256]{1,0:T(8,128)(2,1)S(1)} copy-done((bf16[1792,256]{1,0:T(8,128)(2,1)S(1)}, bf16[1792,256]{1,0:T(8,128)(2,1)}, u32[]{:S(2)}) %copy-start) | copy-done | bytes 917528
  8.4 6.5 %fusion = f32[2048,256]{0,1:T(8,128)} fusion(bf16[2048,1792]{1,0:T(8,128)(2,1)} %param.4, bf16[1792,256]{1,0:T(8,128)(2,1)S(1)} %copy-done), kind=kOutput, calls=%fused_computation.7 | convolution fusion | flops 1879048192 | bytes 10354688 | tf_op jit(solution)/shard_map/dot_general | solution.py:22
  14.9 0.0 reduce-scatter.2.cloned.1.call-update
  14.9 0.0 copy-done.2
  15.0 0.3 copy.11
  15.3 0.0 copy-done.5
  15.3 0.6 dynamic-slice
  16.6 0.0 copy-done.4
  16.6 0.2 dynamic-update-slice
  16.8 5.1 %convert_reduce_fusion = f32[256]{0:T(256)S(1)} fusion(s32[2048,8]{1,0:T(8,128)S(1)} %copy.11), kind=kLoop, calls=%fused_computation | loop fusion | flops 12582656 | bytes 66560 | tf_op jit(solution)/shard_map/reduce_sum | solution.py:14
  21.9 23.1 %psum.7 = f32[256]{0:T(256)S(1)} all-reduce(f32[256]{0:T(256)S(1)} %convert_reduce_fusion), channel_id=1, replica_groups=mesh['tok'=8,'exp'=4] {'tok'}, use_global_device_ids=true, to_apply=%region_5.6 | all-reduce | flops 256 | bytes 2048 | tf_op jit(solution)/shard_map/psum | solution.py:32
  45.0 0.0 copy-start.3
  45.0 5.7 %all-reduce = f32[256]{0:T(256)S(1)} all-reduce(f32[256]{0:T(256)S(1)} %dynamic-update-slice), channel_id=1, replica_groups=mesh['tok'=8,'exp'=4] {'exp'}, use_global_device_ids=true, to_apply=%add | all-reduce | flops 256 | bytes 2048
  50.7 0.6 multiply_add_fusion
  51.3 0.0 reduce-scatter.2.cloned.1.call-done
  51.3 1.2 %add_divide_fusion = f32[2048,64]{0,1:T(8,128)S(1)} fusion(f32[2048,64]{0,1:T(8,128)} %reduce-scatter.2.cloned.1.call-done), kind=kLoop, calls=%fused_computation.3 | loop fusion | flops 393216 | bytes 1048576 | tf_op jit(solution)/shard_map/div | solution.py:24
  52.5 0.0 copy-start.1
  52.5 0.6 select_reduce_fusion
  53.1 6.0 %all-gather = f32[8192,8]{0,1:T(8,128)S(1)} all-gather(f32[2048,8]{0,1:T(8,128)S(1)} %select_reduce_fusion), channel_id=2, replica_groups=mesh['tok'=8,'exp'=4] {'exp'}, dimensions={0}, use_global_device_ids=true | all-gather | bytes 327680 | tf_op jit(solution)/shard_map/all_gather | solution.py:8
  59.1 0.1 reduce.1
  59.2 0.6 multiply_divide_fusion
  59.9 0.0 copy-done.3
  59.9 0.0 copy-done.1
  (5 shorter events, 0.1 us)
Async XLA Ops:
  7.2 1.2 %copy-start = (bf16[1792,256]{1,0:T(8,128)(2,1)S(1)}, bf16[1792,256]{1,0:T(8,128)(2,1)}, u32[]{:S(2)}) copy-start(bf16[1792,256]{1,0:T(8,128)(2,1)} %param.5) | copy-start | bytes 2752516
  7.2 8.1 %copy-start.5 = (u32[32]{0:T(128)S(1)}, u32[32]{0:T(128)}, u32[]{:S(2)}) copy-start(u32[32]{0:T(128)} %constant.20) | copy-start | bytes 388
  7.2 7.8 %copy-start.2 = (s32[2048,8]{0,1:T(8,128)S(1)}, s32[2048,8]{0,1:T(8,128)}, u32[]{:S(2)}) copy-start(s32[2048,8]{0,1:T(8,128)} %param.6) | copy-start | bytes 196612
  7.2 9.4 %copy-start.4 = (f32[64]{0:T(128)S(1)}, f32[64]{0:T(128)}, u32[]{:S(2)}) copy-start(f32[64]{0:T(128)} %param.7) | copy-start | bytes 772
  7.2 44.1 %reduce-scatter.2.cloned.1.call-start = ((), (), s32[]{:S(2)}) async-start(), calls=%async_computation.1 | async-start | bytes 2621440 | tf_op jit(solution)/shard_map/reduce_scatter | solution.py:23
  45.0 14.8 %copy-start.3 = (f32[256]{0:T(256)}, f32[256]{0:T(256)S(1)}, u32[]{:S(2)}) copy-start(f32[256]{0:T(256)S(1)} %psum.7) | copy-start | bytes 3076
  52.5 7.4 %copy-start.1 = (f32[2048,64]{0,1:T(8,128)}, f32[2048,64]{0,1:T(8,128)S(1)}, u32[]{:S(2)}) copy-start(f32[2048,64]{0,1:T(8,128)S(1)} %add_divide_fusion) | copy-start | bytes 1572868
Sparse Core Ops, SparseCore 0:
  15.1 33.9 reduce-scatter.1
